TPU v7x, 32 devices: a whole 2x2x4 slice. The times are simulated.
32 devices in a mesh: groups: 2 (over y), rows: 4 (over z), cols: 2 (over x), sub: 2 (over core).
Axes of the slice: x: 2, y: 2, z: 4, core: 2. Of those that a mesh axis runs over, the one named last changes fastest.
Arguments:
- returns: float32 [8, 64, 8192], P('groups', 'rows', ('cols', 'sub')), parts along dimension 0, may hold values from -6 to 6
- starts: int32 [8, 8192], P('groups', ('cols', 'sub')), parts along dimension 0, may hold values from 0 to 32
- start_block: float32 [8, 32, 8192], P('groups', None, ('cols', 'sub')), parts along dimension 0, may hold values from -6 to 6
Outputs:
- loadings: float32 [8, 32, 8192], P('groups', None, ('cols', 'sub')), parts along dimension 0
There are 2 independent parts, one for each index of `groups`. A program takes and returns all parts, laid end to end along the dimension named above; each array names one. Nothing has to cross between parts.
Inputs may be any that keep to these rules, and one draw needn't show every extreme that they name: `starts`: days before an asset's start day hold returns that do not count.
All inputs are finite; a program needn't handle non-finite values.
Results may differ from a plain program's by a relative error of at most 0.0078.
Values may be sent and summed in bfloat16 or wider, within the bound.
A program may use at most 64 MiB of HBM per device.

v0:
```python
import jax
import jax.numpy as jnp
from jax import lax
from jax.sharding import PartitionSpec as P

ASSETS = 8192
ITERS = 3


def gram_of(image):
    return jnp.einsum("wkj,wlj->wkl", image, image, precision=lax.Precision.HIGHEST)


def project(factors, scaled):
    rounded = factors.astype(jnp.bfloat16)
    return jnp.einsum("wka,wta->wkt", rounded, scaled, preferred_element_type=jnp.float32)


def expand(proj, widened):
    return jnp.einsum("wkt,wta->wka", proj, widened, precision=lax.Precision.HIGHEST)


def orthonormal(image, gram):
    lower = jnp.linalg.cholesky(gram / ASSETS)
    return jax.scipy.linalg.solve_triangular(lower, image, lower=True)


def on_device(returns, starts, start_block):
    windows, days, width = returns.shape
    rows_count = lax.axis_size("rows")
    row_pos = lax.axis_index("rows")
    total_days = days * rows_count
    day_index = row_pos * days + jnp.arange(days, dtype=jnp.int32)
    live = (day_index[None, :, None] >= starts[:, None, :]).astype(jnp.float32)
    counts = (total_days - starts).astype(jnp.float32)
    masked = live * returns
    sums = lax.psum(jnp.sum(masked, axis=1), "rows")
    mean = sums / counts
    centered = live * (returns - mean[:, None, :])
    squares = lax.psum(jnp.sum(centered * centered, axis=1), "rows")
    scaled = (centered * lax.rsqrt(squares + 1.0)[:, None, :]).astype(jnp.bfloat16)
    widened = scaled.astype(jnp.float32)
    factors = start_block
    for step in range(ITERS):
        proj = lax.psum(project(factors, scaled), ("cols", "sub"))
        image = lax.psum(expand(proj, widened), "rows")
        gram = lax.psum(gram_of(image), ("cols", "sub"))
        factors = orthonormal(image, gram)
    return factors


def solution(mesh):
    placed = (
        P("groups", "rows", ("cols", "sub")),
        P("groups", ("cols", "sub")),
        P("groups", None, ("cols", "sub")),
    )
    return jax.shard_map(
        on_device,
        mesh=mesh,
        in_specs=placed,
        out_specs=P("groups", None, ("cols", "sub")),
        check_vma=False,
    )
```

profile of v0, /device:TPU:0, one launch (start us, length us, event | category | flops | bytes accessed | tf_op | source)
XLA Modules:
  0.0 354.8 jit_solution(6312155068273593770)
XLA Ops:
  6.5 0.0 all-reduce.4.cloned.1.call-start
  6.5 1.3 fusion
  7.8 0.0 copy-start.4
  7.9 20.9 %psum.77 = f32[4,2048]{1,0:T(4,128)S(1)} all-reduce(f32[4,2048]{1,0:T(4,128)S(1)} %fusion), channel_id=1, replica_groups=mesh['groups'=2,'rows'=4,'cols'=2,'sub'=2] {'rows'}, use_global_device_ids=true, to_apply=%region_1.0 | all-reduce | flops 8192 | bytes 65536 | tf_op jit(solution)/shard_map/psum | solution.py:37
  28.9 0.2 multiply_reduce_fusion
  29.1 15.8 %psum.78 = f32[4,2048]{1,0:T(4,128)S(1)} all-reduce(f32[4,2048]{1,0:T(4,128)S(1)} %multiply_reduce_fusion), channel_id=1, replica_groups=mesh['groups'=2,'rows'=4,'cols'=2,'sub'=2] {'rows'}, use_global_device_ids=true, to_apply=%region_3.0 | all-reduce | flops 8192 | bytes 65536 | tf_op jit(solution)/shard_map/psum | solution.py:40
  44.9 0.2 multiply_convert_fusion
  45.1 0.2 convolution_bitcast_fusion
  45.3 10.3 %psum.79 = f32[4,32,16]{1,2,0:T(8,128)S(1)} all-reduce(f32[4,32,16]{1,2,0:T(8,128)S(1)} %convolution_bitcast_fusion), channel_id=1, replica_groups=mesh['groups'=2,'rows'=4,'cols'=2,'sub'=2] {'cols','sub'}, use_global_device_ids=true, to_apply=%region_4.0 | all-reduce | flops 2048 | bytes 16384 | tf_op jit(solution)/shard_map/psum | solution.py:45
  55.6 1.6 fusion.9
  57.2 0.0 all-reduce.4.cloned.1.call-update
  57.2 0.0 all-reduce.6.cloned.1.call-start
  57.3 51.6 %all-reduce.4.cloned.1.call-done = f32[4,32,2048]{2,1,0:T(8,128)} async-done(((f32[4,32,2048]{2,1,0:T(8,128)}), f32[4,32,2048]{2,1,0:T(8,128)}) %all-reduce.4.cloned.1.call-update) | async-done | bytes 1048592 | tf_op jit(solution)/shard_map/psum | solution.py:46
  108.8 2.7 fusion.10
  111.6 11.8 %psum.81 = f32[4,32,32]{1,2,0:T(8,128)S(1)} all-reduce(f32[4,32,32]{1,2,0:T(8,128)S(1)} %fusion.10), channel_id=1, replica_groups=mesh['groups'=2,'rows'=4,'cols'=2,'sub'=2] {'cols','sub'}, use_global_device_ids=true, to_apply=%region_6.0 | all-reduce | flops 4096 | bytes 32768 | tf_op jit(solution)/shard_map/psum | solution.py:47
  123.4 0.1 copy.12
  123.6 11.7 %custom-call.10 = f32[4,32,32]{2,1,0:T(8,128)S(1)} custom-call(f32[4,32,32]{2,1,0:T(8,128)S(1)} %fusion.8), custom_call_target="Cholesky" | custom-call | tf_op jit(solution)/shard_map/jit(cholesky)/cholesky | solution.py:24
  135.3 0.1 compare_reduce_fusion.2
  135.4 0.1 select_bitcast_fusion.2
  135.5 9.8 %custom-call.11 = f32[4,1,32,32]{2,3,1,0:T(8,128)S(1)} custom-call(f32[4,1,32,32]{3,2,1,0:T(8,128)S(1)} %select_bitcast_fusion.2), custom_call_target="InvertDiagBlocksLowerTriangular" | custom-call | tf_op jit(solution)/shard_map/jit(_solve_triangular)/vmap()/triangular_solve | solution.py:25
  145.4 1.1 convolution_convert_fusion.1
  146.4 0.2 fusion.11
  146.7 10.5 %psum.82 = f32[4,32,16]{1,2,0:T(8,128)S(1)} all-reduce(f32[4,32,16]{1,2,0:T(8,128)S(1)} %fusion.11), channel_id=1, replica_groups=mesh['groups'=2,'rows'=4,'cols'=2,'sub'=2] {'cols','sub'}, use_global_device_ids=true, to_apply=%region_9.0 | all-reduce | flops 2048 | bytes 16384 | tf_op jit(solution)/shard_map/psum | solution.py:45
  157.2 1.6 fusion.12
  158.8 0.0 all-reduce.6.cloned.1.call-update
  158.8 0.0 all-reduce.8.cloned.1.call-start
  158.8 50.5 %all-reduce.6.cloned.1.call-done = f32[4,32,2048]{2,1,0:T(8,128)} async-done(((f32[4,32,2048]{2,1,0:T(8,128)}), f32[4,32,2048]{2,1,0:T(8,128)}) %all-reduce.6.cloned.1.call-update) | async-done | bytes 1048592 | tf_op jit(solution)/shard_map/psum | solution.py:46
  209.3 2.7 fusion.13
  212.0 11.8 %psum.84 = f32[4,32,32]{1,2,0:T(8,128)S(1)} all-reduce(f32[4,32,32]{1,2,0:T(8,128)S(1)} %fusion.13), channel_id=1, replica_groups=mesh['groups'=2,'rows'=4,'cols'=2,'sub'=2] {'cols','sub'}, use_global_device_ids=true, to_apply=%region_11.0 | all-reduce | flops 4096 | bytes 32768 | tf_op jit(solution)/shard_map/psum | solution.py:47
  223.9 0.1 copy.14
  224.0 11.7 %custom-call.12 = f32[4,32,32]{2,1,0:T(8,128)S(1)} custom-call(f32[4,32,32]{2,1,0:T(8,128)S(1)} %fusion.6), custom_call_target="Cholesky" | custom-call | tf_op jit(solution)/shard_map/jit(cholesky)/cholesky | solution.py:24
  235.8 0.1 compare_reduce_fusion.1
  235.9 0.1 select_bitcast_fusion.1
  236.0 9.8 %custom-call.13 = f32[4,1,32,32]{2,3,1,0:T(8,128)S(1)} custom-call(f32[4,1,32,32]{3,2,1,0:T(8,128)S(1)} %select_bitcast_fusion.1), custom_call_target="InvertDiagBlocksLowerTriangular" | custom-call | tf_op jit(solution)/shard_map/jit(_solve_triangular)/vmap()/triangular_solve | solution.py:25
  245.8 1.1 convolution_convert_fusion
  246.9 0.2 fusion.14
  247.1 10.5 %psum.85 = f32[4,32,16]{1,2,0:T(8,128)S(1)} all-reduce(f32[4,32,16]{1,2,0:T(8,128)S(1)} %fusion.14), channel_id=1, replica_groups=mesh['groups'=2,'rows'=4,'cols'=2,'sub'=2] {'cols','sub'}, use_global_device_ids=true, to_apply=%region_12.0 | all-reduce | flops 2048 | bytes 16384 | tf_op jit(solution)/shard_map/psum | solution.py:45
  257.6 1.6 fusion.15
  259.2 0.0 all-reduce.8.cloned.1.call-update
  259.2 50.5 %all-reduce.8.cloned.1.call-done = f32[4,32,2048]{2,1,0:T(8,128)} async-done(((f32[4,32,2048]{2,1,0:T(8,128)}), f32[4,32,2048]{2,1,0:T(8,128)}) %all-reduce.8.cloned.1.call-update) | async-done | bytes 1048592 | tf_op jit(solution)/shard_map/psum | solution.py:46
  309.7 2.7 fusion.16
  312.5 11.8 %psum.87 = f32[4,32,32]{1,2,0:T(8,128)S(1)} all-reduce(f32[4,32,32]{1,2,0:T(8,128)S(1)} %fusion.16), channel_id=1, replica_groups=mesh['groups'=2,'rows'=4,'cols'=2,'sub'=2] {'cols','sub'}, use_global_device_ids=true, to_apply=%region_14.17 | all-reduce | flops 4096 | bytes 32768 | tf_op jit(solution)/shard_map/psum | solution.py:47
  324.4 0.1 copy.16
  324.5 11.7 %custom-call.14 = f32[4,32,32]{2,1,0:T(8,128)S(1)} custom-call(f32[4,32,32]{2,1,0:T(8,128)S(1)} %fusion.4), custom_call_target="Cholesky" | custom-call | tf_op jit(solution)/shard_map/jit(cholesky)/cholesky | solution.py:24
  336.2 0.1 compare_reduce_fusion
  336.3 0.1 select_bitcast_fusion
  336.4 9.8 %custom-call.15 = f32[4,1,32,32]{2,3,1,0:T(8,128)S(1)} custom-call(f32[4,1,32,32]{3,2,1,0:T(8,128)S(1)} %select_bitcast_fusion), custom_call_target="InvertDiagBlocksLowerTriangular" | custom-call | tf_op jit(solution)/shard_map/jit(_solve_triangular)/vmap()/triangular_solve | solution.py:25
  346.3 2.0 fusion.2
  (25 shorter events, 0.2 us)
Async XLA Ops:
  6.5 22.3 %copy-start.3 = (f32[4,16,2048]{2,1,0:T(8,128)S(1)}, f32[4,16,2048]{2,1,0:T(8,128)}, u32[]{:S(2)}) copy-start(f32[4,16,2048]{2,1,0:T(8,128)} %param.6) | copy-start | bytes 1572868
  6.5 102.3 %all-reduce.4.cloned.1.call-start = ((), (), s32[]{:S(2)}) async-start(), calls=%async_computation | async-start | bytes 2097152 | tf_op jit(solution)/shard_map/psum | solution.py:46
  6.5 22.3 %copy-start.5 = (s32[4,2048]{1,0:T(4,128)S(1)}, s32[4,2048]{1,0:T(4,128)}, u32[]{:S(2)}) copy-start(s32[4,2048]{1,0:T(4,128)} %param.7) | copy-start | bytes 98308
  7.8 37.2 %copy-start.4 = (f32[4,32,2048]{2,1,0:T(8,128)S(1)}, f32[4,32,2048]{2,1,0:T(8,128)}, u32[]{:S(2)}) copy-start(f32[4,32,2048]{2,1,0:T(8,128)} %param.8) | copy-start | bytes 3145732
  57.2 152.1 %all-reduce.6.cloned.1.call-start = ((), (), s32[]{:S(2)}) async-start(), calls=%async_computation.1 | async-start | bytes 2097152 | tf_op jit(solution)/shard_map/psum | solution.py:46
  108.8 36.5 %copy-start = (f32[4,32,2048]{2,1,0:T(8,128)S(1)}, f32[4,32,2048]{2,1,0:T(8,128)}, u32[]{:S(2)}) copy-start(f32[4,32,2048]{2,1,0:T(8,128)} %all-reduce.4.cloned.1.call-done) | copy-start | bytes 3145732
  158.8 151.0 %all-reduce.8.cloned.1.call-start = ((), (), s32[]{:S(2)}) async-start(), calls=%async_computation.2 | async-start | bytes 2097152 | tf_op jit(solution)/shard_map/psum | solution.py:46
  209.3 36.5 %copy-start.1 = (f32[4,32,2048]{2,1,0:T(8,128)S(1)}, f32[4,32,2048]{2,1,0:T(8,128)}, u32[]{:S(2)}) copy-start(f32[4,32,2048]{2,1,0:T(8,128)} %all-reduce.6.cloned.1.call-done) | copy-start | bytes 3145732
  309.7 36.5 %copy-start.2 = (f32[4,32,2048]{2,1,0:T(8,128)S(1)}, f32[4,32,2048]{2,1,0:T(8,128)}, u32[]{:S(2)}) copy-start(f32[4,32,2048]{2,1,0:T(8,128)} %all-reduce.8.cloned.1.call-done) | copy-start | bytes 3145732
Sparse Core Ops, SparseCore 0:
  57.3 51.4 all-reduce.3
  158.9 50.3 all-reduce.5
  259.3 50.3 all-reduce.7
where the time goes:
time: 355 us
  waiting for transfers between devices  153 us (43%)
  blocking collectives  103 us (29%)
  other arithmetic  67.2 us (19%)
  matrix products  17.9 us (5%)
  between operations  13.4 us (4%)
    psum x3, waiting for transfers between devices, on_device(): image = lax.psum(expand(proj, widened), 'rows')  153 us
    another operation x10, other arithmetic, orthonormal(): lower = jnp.linalg.cholesky(gram / ASSETS)  35.6 us
    psum x3, blocking collectives, on_device(): gram = lax.psum(gram_of(image), ('cols', 'sub'))  35.5 us
    psum x3, blocking collectives, on_device(): proj = lax.psum(project(factors, scaled), ('cols', 'sub'))  31.2 us
    another operation x7, other arithmetic, orthonormal(): return jax.scipy.linalg.solve_triangular(lower, image, lower=True)  29.8 us
    psum x1, blocking collectives, on_device(): sums = lax.psum(jnp.sum(masked, axis=1), 'rows')  20.9 us
    psum x1, blocking collectives, on_device(): squares = lax.psum(jnp.sum(centered * centered, axis=1), 'rows')  15.8 us
    dot_general x3, matrix products, gram_of(): jnp.einsum('wkj,wlj->wkl', image, image, precision=lax.Precision.HIGHEST)  8.19 us
  transfers between devices with their start and end apart: 3, of which 3 were waited for; matrix products, arithmetic and copies ran while one was open for 0% of the time, Pallas kernels for 0%

commit v1 on v0

--- a/solution.py
+++ b/solution.py
@@ -42,7 +42,7 @@
     widened = scaled.astype(jnp.float32)
     factors = start_block
     for step in range(ITERS):
-        proj = lax.psum(project(factors, scaled), ("cols", "sub"))
+        proj = jnp.sum(lax.all_gather(project(factors, scaled), ("cols", "sub")), axis=0)
         image = lax.psum(expand(proj, widened), "rows")
         gram = lax.psum(gram_of(image), ("cols", "sub"))
         factors = orthonormal(image, gram)

time: 355 us -> 340 us (0.958)
  blocking collectives: 103 us -> 88.5 us
    psum x3 -> x0, blocking collectives: 31.2 us -> none  [on_device(): proj = lax.psum(project(factors, scaled), ('cols', 'sub'))]
    all_gather x0 -> x3, blocking collectives: none -> 16.3 us  [on_device(): lax.all_gather(project(factors, scaled), ('cols', 'sub'))]
where the time goes in v1:
time: 340 us
  waiting for transfers between devices  152 us (45%)
  blocking collectives  88.5 us (26%)
  other arithmetic  67.2 us (20%)
  matrix products  17.9 us (5%)
  between operations  13.3 us (4%)
    psum x3, waiting for transfers between devices, on_device(): image = lax.psum(expand(proj, widened), 'rows')  152 us
    another operation x10, other arithmetic, orthonormal(): lower = jnp.linalg.cholesky(gram / ASSETS)  35.6 us
    psum x3, blocking collectives, on_device(): gram = lax.psum(gram_of(image), ('cols', 'sub'))  35.5 us
    another operation x7, other arithmetic, orthonormal(): return jax.scipy.linalg.solve_triangular(lower, image, lower=True)  29.8 us
    psum x1, blocking collectives, on_device(): sums = lax.psum(jnp.sum(masked, axis=1), 'rows')  20.9 us
    all_gather x3, blocking collectives, on_device(): lax.all_gather(project(factors, scaled), ('cols', 'sub'))  16.3 us
    psum x1, blocking collectives, on_device(): squares = lax.psum(jnp.sum(centered * centered, axis=1), 'rows')  15.8 us
    dot_general x3, matrix products, gram_of(): jnp.einsum('wkj,wlj->wkl', image, image, precision=lax.Precision.HIGHEST)  8.19 us
  transfers between devices with their start and end apart: 3, of which 3 were waited for; matrix products, arithmetic and copies ran while one was open for 0% of the time, Pallas kernels for 0%

profile of v1, /device:TPU:0, one launch (start us, length us, event | category | flops | bytes accessed | tf_op | source)
XLA Modules:
  0.0 339.6 jit_solution(6191245718169102917)
XLA Ops:
  6.5 0.0 all-reduce.4.cloned.1.call-start
  6.5 1.3 fusion
  7.8 0.0 copy-start.4
  7.9 20.9 %psum.56 = f32[4,2048]{1,0:T(4,128)S(1)} all-reduce(f32[4,2048]{1,0:T(4,128)S(1)} %fusion), channel_id=1, replica_groups=mesh['groups'=2,'rows'=4,'cols'=2,'sub'=2] {'rows'}, use_global_device_ids=true, to_apply=%region_1.0 | all-reduce | flops 8192 | bytes 65536 | tf_op jit(solution)/shard_map/psum | solution.py:37
  28.9 0.2 multiply_reduce_fusion
  29.1 15.8 %psum.57 = f32[4,2048]{1,0:T(4,128)S(1)} all-reduce(f32[4,2048]{1,0:T(4,128)S(1)} %multiply_reduce_fusion), channel_id=1, replica_groups=mesh['groups'=2,'rows'=4,'cols'=2,'sub'=2] {'rows'}, use_global_device_ids=true, to_apply=%region_3.0 | all-reduce | flops 8192 | bytes 65536 | tf_op jit(solution)/shard_map/psum | solution.py:40
  44.9 0.2 multiply_convert_fusion
  45.1 0.2 convolution_bitcast_fusion
  45.3 5.4 %all-gather = f32[16,32,16]{1,2,0:T(8,128)S(1)} all-gather(f32[4,32,16]{1,2,0:T(8,128)S(1)} %convolution_bitcast_fusion), channel_id=2, replica_groups=mesh['groups'=2,'rows'=4,'cols'=2,'sub'=2] {'cols','sub'}, dimensions={0}, use_global_device_ids=true | all-gather | bytes 40960 | tf_op jit(solution)/shard_map/all_gather | solution.py:45
  50.8 1.6 fusion.9
  52.3 0.0 all-reduce.4.cloned.1.call-update
  52.4 0.0 all-reduce.6.cloned.1.call-start
  52.4 51.4 %all-reduce.4.cloned.1.call-done = f32[4,32,2048]{2,1,0:T(8,128)} async-done(((f32[4,32,2048]{2,1,0:T(8,128)}), f32[4,32,2048]{2,1,0:T(8,128)}) %all-reduce.4.cloned.1.call-update) | async-done | bytes 1048592 | tf_op jit(solution)/shard_map/psum | solution.py:46
  103.9 2.7 fusion.10
  106.6 11.8 %psum.59 = f32[4,32,32]{1,2,0:T(8,128)S(1)} all-reduce(f32[4,32,32]{1,2,0:T(8,128)S(1)} %fusion.10), channel_id=1, replica_groups=mesh['groups'=2,'rows'=4,'cols'=2,'sub'=2] {'cols','sub'}, use_global_device_ids=true, to_apply=%region_6.0 | all-reduce | flops 4096 | bytes 32768 | tf_op jit(solution)/shard_map/psum | solution.py:47
  118.5 0.1 copy.19
  118.6 11.7 %custom-call.10 = f32[4,32,32]{2,1,0:T(8,128)S(1)} custom-call(f32[4,32,32]{2,1,0:T(8,128)S(1)} %fusion.8), custom_call_target="Cholesky" | custom-call | tf_op jit(solution)/shard_map/jit(cholesky)/cholesky | solution.py:24
  130.3 0.1 compare_reduce_fusion.2
  130.5 0.1 select_bitcast_fusion.2
  130.5 9.8 %custom-call.11 = f32[4,1,32,32]{2,3,1,0:T(8,128)S(1)} custom-call(f32[4,1,32,32]{3,2,1,0:T(8,128)S(1)} %select_bitcast_fusion.2), custom_call_target="InvertDiagBlocksLowerTriangular" | custom-call | tf_op jit(solution)/shard_map/jit(_solve_triangular)/vmap()/triangular_solve | solution.py:25
  140.4 1.1 convolution_convert_fusion.1
  141.5 0.2 fusion.11
  141.7 5.4 %all-gather.1 = f32[16,32,16]{1,2,0:T(8,128)S(1)} all-gather(f32[4,32,16]{1,2,0:T(8,128)S(1)} %fusion.11), channel_id=3, replica_groups=mesh['groups'=2,'rows'=4,'cols'=2,'sub'=2] {'cols','sub'}, dimensions={0}, use_global_device_ids=true | all-gather | bytes 40960 | tf_op jit(solution)/shard_map/all_gather | solution.py:45
  147.2 1.6 fusion.12
  148.7 0.0 all-reduce.6.cloned.1.call-update
  148.8 0.0 all-reduce.8.cloned.1.call-start
  148.8 50.4 %all-reduce.6.cloned.1.call-done = f32[4,32,2048]{2,1,0:T(8,128)} async-done(((f32[4,32,2048]{2,1,0:T(8,128)}), f32[4,32,2048]{2,1,0:T(8,128)}) %all-reduce.6.cloned.1.call-update) | async-done | bytes 1048592 | tf_op jit(solution)/shard_map/psum | solution.py:46
  199.2 2.7 fusion.13
  201.9 11.8 %psum.61 = f32[4,32,32]{1,2,0:T(8,128)S(1)} all-reduce(f32[4,32,32]{1,2,0:T(8,128)S(1)} %fusion.13), channel_id=1, replica_groups=mesh['groups'=2,'rows'=4,'cols'=2,'sub'=2] {'cols','sub'}, use_global_device_ids=true, to_apply=%region_11.0 | all-reduce | flops 4096 | bytes 32768 | tf_op jit(solution)/shard_map/psum | solution.py:47
  213.8 0.1 copy.22
  213.9 11.7 %custom-call.12 = f32[4,32,32]{2,1,0:T(8,128)S(1)} custom-call(f32[4,32,32]{2,1,0:T(8,128)S(1)} %fusion.6), custom_call_target="Cholesky" | custom-call | tf_op jit(solution)/shard_map/jit(cholesky)/cholesky | solution.py:24
  225.7 0.1 compare_reduce_fusion.1
  225.8 0.1 select_bitcast_fusion.1
  225.9 9.8 %custom-call.13 = f32[4,1,32,32]{2,3,1,0:T(8,128)S(1)} custom-call(f32[4,1,32,32]{3,2,1,0:T(8,128)S(1)} %select_bitcast_fusion.1), custom_call_target="InvertDiagBlocksLowerTriangular" | custom-call | tf_op jit(solution)/shard_map/jit(_solve_triangular)/vmap()/triangular_solve | solution.py:25
  235.7 1.1 convolution_convert_fusion
  236.8 0.2 fusion.14
  237.0 5.4 %all-gather.2 = f32[16,32,16]{1,2,0:T(8,128)S(1)} all-gather(f32[4,32,16]{1,2,0:T(8,128)S(1)} %fusion.14), channel_id=4, replica_groups=mesh['groups'=2,'rows'=4,'cols'=2,'sub'=2] {'cols','sub'}, dimensions={0}, use_global_device_ids=true | all-gather | bytes 40960 | tf_op jit(solution)/shard_map/all_gather | solution.py:45
  242.5 1.6 fusion.15
  244.1 0.0 all-reduce.8.cloned.1.call-update
  244.1 50.4 %all-reduce.8.cloned.1.call-done = f32[4,32,2048]{2,1,0:T(8,128)} async-done(((f32[4,32,2048]{2,1,0:T(8,128)}), f32[4,32,2048]{2,1,0:T(8,128)}) %all-reduce.8.cloned.1.call-update) | async-done | bytes 1048592 | tf_op jit(solution)/shard_map/psum | solution.py:46
  294.5 2.7 fusion.16
  297.3 11.8 %psum.63 = f32[4,32,32]{1,2,0:T(8,128)S(1)} all-reduce(f32[4,32,32]{1,2,0:T(8,128)S(1)} %fusion.16), channel_id=1, replica_groups=mesh['groups'=2,'rows'=4,'cols'=2,'sub'=2] {'cols','sub'}, use_global_device_ids=true, to_apply=%region_14.17 | all-reduce | flops 4096 | bytes 32768 | tf_op jit(solution)/shard_map/psum | solution.py:47
  309.1 0.1 copy.25
  309.2 11.7 %custom-call.14 = f32[4,32,32]{2,1,0:T(8,128)S(1)} custom-call(f32[4,32,32]{2,1,0:T(8,128)S(1)} %fusion.4), custom_call_target="Cholesky" | custom-call | tf_op jit(solution)/shard_map/jit(cholesky)/cholesky | solution.py:24
  321.0 0.1 compare_reduce_fusion
  321.1 0.1 select_bitcast_fusion
  321.2 9.8 %custom-call.15 = f32[4,1,32,32]{2,3,1,0:T(8,128)S(1)} custom-call(f32[4,1,32,32]{3,2,1,0:T(8,128)S(1)} %select_bitcast_fusion), custom_call_target="InvertDiagBlocksLowerTriangular" | custom-call | tf_op jit(solution)/shard_map/jit(_solve_triangular)/vmap()/triangular_solve | solution.py:25
  331.0 2.0 fusion.2
  (28 shorter events, 0.3 us)
Async XLA Ops:
  6.5 22.3 %copy-start.3 = (f32[4,16,2048]{2,1,0:T(8,128)S(1)}, f32[4,16,2048]{2,1,0:T(8,128)}, u32[]{:S(2)}) copy-start(f32[4,16,2048]{2,1,0:T(8,128)} %param.6) | copy-start | bytes 1572868
  6.5 97.3 %all-reduce.4.cloned.1.call-start = ((), (), s32[]{:S(2)}) async-start(), calls=%async_computation | async-start | bytes 2097152 | tf_op jit(solution)/shard_map/psum | solution.py:46
  6.5 22.3 %copy-start.5 = (s32[4,2048]{1,0:T(4,128)S(1)}, s32[4,2048]{1,0:T(4,128)}, u32[]{:S(2)}) copy-start(s32[4,2048]{1,0:T(4,128)} %param.7) | copy-start | bytes 98308
  7.8 37.2 %copy-start.4 = (f32[4,32,2048]{2,1,0:T(8,128)S(1)}, f32[4,32,2048]{2,1,0:T(8,128)}, u32[]{:S(2)}) copy-start(f32[4,32,2048]{2,1,0:T(8,128)} %param.8) | copy-start | bytes 3145732
  52.4 146.8 %all-reduce.6.cloned.1.call-start = ((), (), s32[]{:S(2)}) async-start(), calls=%async_computation.1 | async-start | bytes 2097152 | tf_op jit(solution)/shard_map/psum | solution.py:46
  103.9 36.5 %copy-start = (f32[4,32,2048]{2,1,0:T(8,128)S(1)}, f32[4,32,2048]{2,1,0:T(8,128)}, u32[]{:S(2)}) copy-start(f32[4,32,2048]{2,1,0:T(8,128)} %all-reduce.4.cloned.1.call-done) | copy-start | bytes 3145732
  148.8 145.7 %all-reduce.8.cloned.1.call-start = ((), (), s32[]{:S(2)}) async-start(), calls=%async_computation.2 | async-start | bytes 2097152 | tf_op jit(solution)/shard_map/psum | solution.py:46
  199.2 36.5 %copy-start.1 = (f32[4,32,2048]{2,1,0:T(8,128)S(1)}, f32[4,32,2048]{2,1,0:T(8,128)}, u32[]{:S(2)}) copy-start(f32[4,32,2048]{2,1,0:T(8,128)} %all-reduce.6.cloned.1.call-done) | copy-start | bytes 3145732
  294.5 36.5 %copy-start.2 = (f32[4,32,2048]{2,1,0:T(8,128)S(1)}, f32[4,32,2048]{2,1,0:T(8,128)}, u32[]{:S(2)}) copy-start(f32[4,32,2048]{2,1,0:T(8,128)} %all-reduce.8.cloned.1.call-done) | copy-start | bytes 3145732
Sparse Core Ops, SparseCore 0:
  52.5 51.3 all-reduce.3
  148.9 50.2 all-reduce.5
  244.2 50.2 all-reduce.7
